TPU v7x, 32 devices: a whole 2x2x4 slice. The times are simulated.
32 devices in a mesh: section: 2 (over core), dev: 16 (over z, y, x).
Axes of the slice: x: 2, y: 2, z: 4, core: 2. Of those that a mesh axis runs over, the one named last changes fastest.
Arguments:
- indices: int32 [2048, 32, 8], P(('section', 'dev')), may hold values from 0 to 32767
- pool_len: int32 [32], replicated, may hold values from 1 to 8
- tables: bfloat16 [1048576, 128], P(('section', 'dev')), may hold values from -3 to 3
- w_first: bfloat16 [4096, 4096], P('dev', 'section'), may hold values from -0.09375 to 0.09375
- b_first: bfloat16 [4096], P('section'), may hold values from -3 to 3
- w_out: bfloat16 [4096], P('section'), may hold values from -0.09375 to 0.09375
Outputs:
- logits: float32 [2048], P('dev')
Inputs may be any that keep to these rules, and one draw needn't show every extreme that they name: `indices`: ids of rows of the table named by the second index.
All inputs are finite; a program needn't handle non-finite values.
Results may differ from a plain program's by a relative error of at most 0.0095.
Values may be sent and summed in bfloat16 or wider, within the bound.
A program may use at most 128 MiB of HBM per device.

v0:
```python
import jax
import jax.numpy as jnp
from jax import lax
from jax.sharding import PartitionSpec as P


def body(indices, pool_len, tables, w_first, b_first, w_out):
    sec_count = lax.axis_size("section")
    dev_count = lax.axis_size("dev")
    devices = sec_count * dev_count
    dev_rows, n_tables, pool_size = indices.shape
    rows_dev, emb_width = tables.shape
    row_split = devices // n_tables
    position = lax.axis_index("section") * dev_count + lax.axis_index("dev")
    table_id = position // row_split
    first_row = position % row_split * rows_dev
    outgoing = jnp.repeat(indices, row_split, axis=1)
    arrived = lax.all_to_all(outgoing, ("section", "dev"), split_axis=1, concat_axis=0, tiled=True)
    all_rows = devices * dev_rows
    wanted = arrived.reshape(all_rows, pool_size) - first_row
    live_slots = jnp.sum(jnp.where(jnp.arange(n_tables) == table_id, pool_len, 0))
    usable = (wanted >= 0) & (wanted < rows_dev) & (jnp.arange(pool_size)[None, :] < live_slots)
    safe_rows = jnp.where(usable, wanted, 0)
    looked = jnp.take(tables, safe_rows, axis=0)
    picked = jnp.where(usable[:, :, None], looked, jnp.zeros((), jnp.bfloat16))
    partial_value = jnp.sum(picked.astype(jnp.float32), axis=1).astype(jnp.bfloat16)
    ordered = jnp.transpose(
        partial_value.reshape(dev_count, sec_count, dev_rows, emb_width), (1, 0, 2, 3)
    )
    received = lax.all_to_all(
        ordered.reshape(devices, dev_rows, emb_width),
        ("section", "dev"),
        split_axis=0,
        concat_axis=0,
        tiled=True,
    )
    summed = jnp.sum(
        received.reshape(n_tables, row_split, dev_rows, emb_width).astype(jnp.float32), axis=1
    )
    features = jnp.transpose(summed.astype(jnp.bfloat16), (1, 0, 2)).reshape(
        dev_rows, n_tables * emb_width
    )
    samples = lax.all_gather(features, "section", axis=0, tiled=True)
    whole_weights = lax.all_gather(w_first, "dev", axis=0, tiled=True)
    pre_act = jnp.dot(samples, whole_weights, preferred_element_type=jnp.float32)
    hidden = jnp.maximum(pre_act + b_first.astype(jnp.float32)[None, :], 0.0)
    logit_part = jnp.sum(hidden * w_out.astype(jnp.float32)[None, :], axis=1)
    return lax.psum(logit_part, "section")


def solution(mesh):
    placed = (
        P(("section", "dev"), None, None),
        P(),
        P(("section", "dev"), None),
        P("dev", "section"),
        P("section"),
        P("section"),
    )
    return jax.shard_map(body, mesh=mesh, in_specs=placed, out_specs=P("dev"), check_vma=False)
```

profile of v0, /device:TPU:0, one launch (start us, length us, event | category | flops | bytes accessed | tf_op | source)
XLA Modules:
  0.0 337.2 jit_solution(18316282832456618671)
XLA Ops:
  6.5 1.6 reshape.131
  8.2 7.3 %all-to-all-start = ((s32[32,1,512]{2,1,0:T(1,128)}), s32[32,1,512]{2,1,0:T(1,128)S(1)}, u32[]{:S(2)}, u32[]{:S(2)}) async-start(s32[32,1,512]{2,1,0:T(1,128)} %reshape.131), calls=%async_computation | async-start | bytes 131072 | tf_op jit(solution)/shard_map/all_to_all | solution.py:18
  15.5 0.0 all-gather.3.cloned.1.call-start
  15.6 1.3 fusion.5
  16.9 0.6 iota_compare_fusion
  17.5 5.3 %all-to-all-done = s32[32,1,512]{2,1,0:T(1,128)S(1)} async-done(((s32[32,1,512]{2,1,0:T(1,128)}), s32[32,1,512]{2,1,0:T(1,128)S(1)}, u32[]{:S(2)}, u32[]{:S(2)}) %all-to-all-start) | async-done | bytes 65568 | tf_op jit(solution)/shard_map/all_to_all | solution.py:18
  22.8 0.5 broadcast.97
  23.4 0.8 reduce.1
  24.2 0.1 reshape.132
  24.3 0.1 reshape.117
  24.4 0.1 reshape.118
  24.5 0.1 and_and_fusion
  24.6 0.4 copy.14
  25.0 0.4 copy.15
  25.5 0.1 compare_select_fusion
  25.6 0.3 copy.17
  25.9 0.5 reshape.124
  26.4 59.4 %gather_fusion = bf16[16384,128]{1,0:T(8,128)(2,1)} fusion(bf16[32768,128]{1,0:T(8,128)(2,1)} %param.8, s32[16384]{0:T(1024)S(1)} %broadcast_clamp_fusion), kind=kCustom, calls=%fused_computation | custom fusion | bytes 8454144 | tf_op jit(solution)/shard_map/jit(_take)/gather | solution.py:24
  85.8 0.0 copy-start
  85.8 0.0 copy-start.1
  85.8 12.6 %fusion.1 = bf16[2048,128]{1,0:T(8,128)(2,1)S(1)} fusion(bf16[16384,128]{1,0:T(8,128)(2,1)} %gather_fusion, pred[2048,8]{1,0:T(8,128)(4,1)S(1)} %copy.15, pred[2048,8]{1,0:T(8,128)(4,1)S(1)} %copy.14), kind=kLoop, calls=%fused_computation.3 | loop fusion | flops 6029312 | bytes 4751360 | tf_op jit(solution)/shard_map/reduce_sum | solution.py:26
  98.5 18.5 %all_to_all.20 = bf16[32,64,128]{2,1,0:T(8,128)(2,1)S(1)} all-to-all(bf16[32,64,128]{2,1,0:T(8,128)(2,1)S(1)} %bitcast.36), channel_id=1, replica_groups=mesh['section'=2,'dev'=16] {'section','dev'}, dimensions={0} | all-to-all | bytes 1048576 | tf_op jit(solution)/shard_map/all_to_all | solution.py:30
  117.1 0.9 copy_bitcast_fusion
  118.0 0.0 all-gather.3.cloned.1.call-update
  118.0 0.0 all-gather.5.cloned.1.call-start
  118.0 0.7 all-gather.5.cloned.1.call-update
  118.7 0.0 copy-done
  118.8 0.0 copy-done.1
  118.8 5.0 %all-gather.3.cloned.1.call-done = bf16[128,4096]{1,0:T(8,128)(2,1)} async-done(((bf16[64,4096]{1,0:T(8,128)(2,1)}), bf16[128,4096]{1,0:T(8,128)(2,1)}) %all-gather.3.cloned.1.call-update) | async-done | bytes 1048592 | tf_op jit(solution)/shard_map/all_gather | solution.py:43
  123.8 195.0 %all-gather.5.cloned.1.call-done = bf16[4096,2048]{1,0:T(8,128)(2,1)} async-done(((bf16[256,2048]{1,0:T(8,128)(2,1)}), bf16[4096,2048]{1,0:T(8,128)(2,1)}) %all-gather.5.cloned.1.call-update) | async-done | bytes 16777232 | tf_op jit(solution)/shard_map/all_gather | solution.py:44
  318.8 8.6 %fusion.4 = f32[128]{0:T(128)S(1)} fusion(bf16[128,4096]{1,0:T(8,128)(2,1)} %all-gather.3.cloned.1.call-done, bf16[4096,2048]{1,0:T(8,128)(2,1)} %all-gather.5.cloned.1.call-done, f32[2048]{0:T(1024)S(1)} %convert_element_type.12, f32[2048]{0:T(1024)S(1)} %convert_element_type.5), kind=kOutput, calls=%fused_computation.7 | convolution fusion | flops 2148532224 | bytes 17842688 | tf_op jit(solution)/shard_map/dot_general | solution.py:45
  327.4 3.0 psum.7
  (6 shorter events, 0.1 us)
Async XLA Ops:
  8.2 14.7 %all-to-all-start = ((s32[32,1,512]{2,1,0:T(1,128)}), s32[32,1,512]{2,1,0:T(1,128)S(1)}, u32[]{:S(2)}, u32[]{:S(2)}) async-start(s32[32,1,512]{2,1,0:T(1,128)} %reshape.131), calls=%async_computation | async-start | bytes 131072 | tf_op jit(solution)/shard_map/all_to_all | solution.py:18
  15.5 108.3 %all-gather.3.cloned.1.call-start = ((), (), s32[]{:S(2)}) async-start(), calls=%async_computation.2 | async-start | bytes 1572864 | tf_op jit(solution)/shard_map/all_gather | solution.py:43
  85.8 32.9 %copy-start = (bf16[2048]{0:T(1024)(128)(2,1)S(1)}, bf16[2048]{0:T(1024)(128)(2,1)}, u32[]{:S(2)}) copy-start(bf16[2048]{0:T(1024)(128)(2,1)} %param.11) | copy-start | bytes 12292
  85.8 32.9 %copy-start.1 = (bf16[2048]{0:T(1024)(128)(2,1)S(1)}, bf16[2048]{0:T(1024)(128)(2,1)}, u32[]{:S(2)}) copy-start(bf16[2048]{0:T(1024)(128)(2,1)} %param.10) | copy-start | bytes 12292
  118.0 200.8 %all-gather.5.cloned.1.call-start = ((), (), s32[]{:S(2)}) async-start(), calls=%async_computation.3 | async-start | bytes 17825792 | tf_op jit(solution)/shard_map/all_gather | solution.py:44
Sparse Core Ops, SparseCore 0:
  118.1 5.6 all-gather.2
  126.6 192.1 all-gather.4
where the time goes:
time: 337 us
  waiting for transfers between devices  206 us (61%)
  local copies, waits for them, and re-layouts  64.5 us (19%)
  blocking collectives  21.5 us (6%)
  other arithmetic  15.6 us (5%)
  between operations  13.5 us (4%)
  matrix products  8.58 us (3%)
  starting transfers between devices  7.41 us (2%)
    all_gather x1, waiting for transfers between devices, body(): whole_weights = lax.all_gather(w_first, 'dev', axis=0, tiled=True)  195 us
    gather x1, local copies, waits for them, and re-layouts, body(): looked = jnp.take(tables, safe_rows, axis=0)  59.4 us
    all_to_all x1, blocking collectives, body(): lax.all_to_all(ordered.reshape(devices, dev_rows, emb_width), ('section',...  18.5 us
    reduce_sum x1, other arithmetic, body(): jnp.sum(picked.astype(jnp.float32), axis=1).astype(jnp.bfloat16)  12.6 us
    dot_general x1, matrix products, body(): jnp.dot(samples, whole_weights, preferred_element_type=jnp.float32)  8.58 us
    all_to_all x1, starting transfers between devices, body(): lax.all_to_all(outgoing, ('section', 'dev'), split_axis=1, concat_axis=0,...  7.33 us
  transfers between devices with their start and end apart: 3, of which 3 were waited for; matrix products, arithmetic and copies ran while one was open for 1% of the time, Pallas kernels for 0%

commit v1 on v0

--- a/solution.py
+++ b/solution.py
@@ -1,7 +1,22 @@
+import functools
 import jax
 import jax.numpy as jnp
 from jax import lax
 from jax.sharding import PartitionSpec as P
+
+
+def find_the_ranges(vec, comm_axis):
+    axis_len = lax.axis_size(comm_axis)
+    taken_in = [None] * axis_len
+    slots = list(map(lambda j: (j, (j + 1) % axis_len), range(axis_len)))
+    taken_in[axis_len - 1] = vec
+    for w in range(axis_len - 2, -1, -1):
+        taken_in[w] = lax.ppermute(taken_in[w + 1], comm_axis, slots)
+    high = jnp.concatenate(taken_in, axis=0)
+    return jnp.roll(high, (lax.axis_index(comm_axis) + 1) * vec.shape[0], axis=0)
+
+
+measure_terms_up = functools.partial(find_the_ranges, comm_axis="dev")
 
 
 def body(indices, pool_len, tables, w_first, b_first, w_out):
@@ -41,7 +56,7 @@
         dev_rows, n_tables * emb_width
     )
     samples = lax.all_gather(features, "section", axis=0, tiled=True)
-    whole_weights = lax.all_gather(w_first, "dev", axis=0, tiled=True)
+    whole_weights = measure_terms_up(w_first)
     pre_act = jnp.dot(samples, whole_weights, preferred_element_type=jnp.float32)
     hidden = jnp.maximum(pre_act + b_first.astype(jnp.float32)[None, :], 0.0)
     logit_part = jnp.sum(hidden * w_out.astype(jnp.float32)[None, :], axis=1)

time: 337 us -> 521 us (1.55)
  waiting for transfers between devices: 206 us -> 326 us
  local copies, waits for them, and re-layouts: 64.5 us -> 135 us
  blocking collectives: 21.5 us -> 2.97 us
  starting transfers between devices: 7.41 us -> 15.6 us
    ppermute x0 -> x15, waiting for transfers between devices: none -> 283 us  [find_the_ranges(): taken_in[w] = lax.ppermute(taken_in[w + 1], comm_axis, slots)]
    all_gather x1 -> x0, waiting for transfers between devices: 195 us -> none  [body(): whole_weights = lax.all_gather(w_first, 'dev', axis=0, tiled=True)]
    unnamed x6 -> x77, local copies, waits for them, and re-layouts: 1.74 us -> 65.7 us
    all_to_all x0 -> x1, waiting for transfers between devices: none -> 31.9 us  [body(): lax.all_to_all(ordered.reshape(devices, dev_rows, emb_width), ('section',...]
    all_to_all x1 -> x0, blocking collectives: 18.5 us -> none  [body(): lax.all_to_all(ordered.reshape(devices, dev_rows, emb_width), ('section',...]
    all_to_all x1, waiting for transfers between devices: 5.32 us -> 11.2 us  [body(): lax.all_to_all(outgoing, ('section', 'dev'), split_axis=1, concat_axis=0,...]
  transfers between devices with their start and end apart: 3 -> 18, of which waited for: 3 -> 14; matrix products, arithmetic and copies ran while one was open for 1% -> 28% of each run, Pallas kernels for 0% -> 0%
where the time goes in v1:
time: 521 us; the launch traced here: 519 us
  waiting for transfers between devices  326 us (63%)
  local copies, waits for them, and re-layouts  135 us (26%)
  other arithmetic  17 us (3%)
  starting transfers between devices  15.6 us (3%)
  between operations  13.7 us (3%)
  matrix products  8.58 us (2%)
    ppermute x15, waiting for transfers between devices, find_the_ranges(): taken_in[w] = lax.ppermute(taken_in[w + 1], comm_axis, slots)  283 us
    unnamed x77, local copies, waits for them, and re-layouts  65.7 us
    gather x1, local copies, waits for them, and re-layouts, body(): looked = jnp.take(tables, safe_rows, axis=0)  59.9 us
    all_to_all x1, waiting for transfers between devices, body(): lax.all_to_all(ordered.reshape(devices, dev_rows, emb_width), ('section',...  31.9 us
    reduce_sum x1, other arithmetic, body(): jnp.sum(picked.astype(jnp.float32), axis=1).astype(jnp.bfloat16)  12.8 us
    all_to_all x1, waiting for transfers between devices, body(): lax.all_to_all(outgoing, ('section', 'dev'), split_axis=1, concat_axis=0,...  11.2 us
  transfers between devices with their start and end apart: 18, of which 14 were waited for; matrix products, arithmetic and copies ran while one was open for 28% of the time, Pallas kernels for 0%

profile of v1, /device:TPU:0, one launch (start us, length us, event | category | flops | bytes accessed | tf_op | source)
XLA Modules:
  0.0 519.5 jit_solution(1589710731771580113)
XLA Ops:
  6.5 3.0 collective-permute-start
  9.5 27.4 %collective-permute-done = bf16[256,2048]{1,0:T(8,128)(2,1)S(1)} collective-permute-done((bf16[256,2048]{1,0:T(8,128)(2,1)}, bf16[256,2048]{1,0:T(8,128)(2,1)S(1)}, u32[]{:S(2)}, u32[]{:S(2)}) %collective-permute-start) | collective-permute-done | bytes 1048608 | tf_op jit(solution)/shard_map/ppermute | solution.py:14
  36.9 27.9 %collective-permute-done.1 = bf16[256,2048]{1,0:T(8,128)(2,1)S(1)} collective-permute-done((bf16[256,2048]{1,0:T(8,128)(2,1)S(1)}, bf16[256,2048]{1,0:T(8,128)(2,1)S(1)}, u32[]{:S(2)}, u32[]{:S(2)}) %collective-permute-start.1) | collective-permute-done | bytes 1048608 | tf_op jit(solution)/shard_map/ppermute | solution.py:14
  64.8 27.1 %collective-permute-done.2 = bf16[256,2048]{1,0:T(8,128)(2,1)S(1)} collective-permute-done((bf16[256,2048]{1,0:T(8,128)(2,1)S(1)}, bf16[256,2048]{1,0:T(8,128)(2,1)S(1)}, u32[]{:S(2)}, u32[]{:S(2)}) %collective-permute-start.2) | collective-permute-done | bytes 1048608 | tf_op jit(solution)/shard_map/ppermute | solution.py:14
  92.8 26.2 %collective-permute-done.3 = bf16[256,2048]{1,0:T(8,128)(2,1)S(1)} collective-permute-done((bf16[256,2048]{1,0:T(8,128)(2,1)S(1)}, bf16[256,2048]{1,0:T(8,128)(2,1)S(1)}, u32[]{:S(2)}, u32[]{:S(2)}) %collective-permute-start.3) | collective-permute-done | bytes 1048608 | tf_op jit(solution)/shard_map/ppermute | solution.py:14
  120.0 25.3 %collective-permute-done.4 = bf16[256,2048]{1,0:T(8,128)(2,1)S(1)} collective-permute-done((bf16[256,2048]{1,0:T(8,128)(2,1)S(1)}, bf16[256,2048]{1,0:T(8,128)(2,1)S(1)}, u32[]{:S(2)}, u32[]{:S(2)}) %collective-permute-start.4) | collective-permute-done | bytes 1048608 | tf_op jit(solution)/shard_map/ppermute | solution.py:14
  145.4 1.0 copy-done.5
  146.4 24.5 %collective-permute-done.5 = bf16[256,2048]{1,0:T(8,128)(2,1)S(1)} collective-permute-done((bf16[256,2048]{1,0:T(8,128)(2,1)S(1)}, bf16[256,2048]{1,0:T(8,128)(2,1)S(1)}, u32[]{:S(2)}, u32[]{:S(2)}) %collective-permute-start.5) | collective-permute-done | bytes 1048608 | tf_op jit(solution)/shard_map/ppermute | solution.py:14
  171.8 23.6 %collective-permute-done.6 = bf16[256,2048]{1,0:T(8,128)(2,1)S(1)} collective-permute-done((bf16[256,2048]{1,0:T(8,128)(2,1)S(1)}, bf16[256,2048]{1,0:T(8,128)(2,1)S(1)}, u32[]{:S(2)}, u32[]{:S(2)}) %collective-permute-start.6) | collective-permute-done | bytes 1048608 | tf_op jit(solution)/shard_map/ppermute | solution.py:14
  195.5 1.0 copy-done.9
  196.5 22.8 %collective-permute-done.7 = bf16[256,2048]{1,0:T(8,128)(2,1)S(1)} collective-permute-done((bf16[256,2048]{1,0:T(8,128)(2,1)S(1)}, bf16[256,2048]{1,0:T(8,128)(2,1)S(1)}, u32[]{:S(2)}, u32[]{:S(2)}) %collective-permute-start.7) | collective-permute-done | bytes 1048608 | tf_op jit(solution)/shard_map/ppermute | solution.py:14
  220.2 22.3 %collective-permute-done.8 = bf16[256,2048]{1,0:T(8,128)(2,1)S(1)} collective-permute-done((bf16[256,2048]{1,0:T(8,128)(2,1)S(1)}, bf16[256,2048]{1,0:T(8,128)(2,1)S(1)}, u32[]{:S(2)}, u32[]{:S(2)}) %collective-permute-start.8) | collective-permute-done | bytes 1048608 | tf_op jit(solution)/shard_map/ppermute | solution.py:14
  242.5 1.1 copy-done.13
  243.5 22.4 %collective-permute-done.9 = bf16[256,2048]{1,0:T(8,128)(2,1)S(1)} collective-permute-done((bf16[256,2048]{1,0:T(8,128)(2,1)S(1)}, bf16[256,2048]{1,0:T(8,128)(2,1)S(1)}, u32[]{:S(2)}, u32[]{:S(2)}) %collective-permute-start.9) | collective-permute-done | bytes 1048608 | tf_op jit(solution)/shard_map/ppermute | solution.py:14
  266.9 23.3 %collective-permute-done.10 = bf16[256,2048]{1,0:T(8,128)(2,1)S(1)} collective-permute-done((bf16[256,2048]{1,0:T(8,128)(2,1)S(1)}, bf16[256,2048]{1,0:T(8,128)(2,1)S(1)}, u32[]{:S(2)}, u32[]{:S(2)}) %collective-permute-start.10) | collective-permute-done | bytes 1048608 | tf_op jit(solution)/shard_map/ppermute | solution.py:14
  290.2 1.8 reshape.131
  292.0 5.9 %all-to-all-start = ((s32[32,1,512]{2,1,0:T(1,128)}), s32[32,1,512]{2,1,0:T(1,128)S(1)}, u32[]{:S(2)}, u32[]{:S(2)}) async-start(s32[32,1,512]{2,1,0:T(1,128)} %reshape.131), calls=%async_computation | async-start | bytes 131072 | tf_op jit(solution)/shard_map/all_to_all | solution.py:33
  297.8 1.3 fusion.16
  299.8 11.2 %all-to-all-done = s32[32,1,512]{2,1,0:T(1,128)S(1)} async-done(((s32[32,1,512]{2,1,0:T(1,128)}), s32[32,1,512]{2,1,0:T(1,128)S(1)}, u32[]{:S(2)}, u32[]{:S(2)}) %all-to-all-start) | async-done | bytes 65568 | tf_op jit(solution)/shard_map/all_to_all | solution.py:33
  313.5 1.2 copy.14
  314.7 1.1 copy.15
  316.5 1.3 copy.17
  317.8 1.6 reshape.124
  319.5 59.9 %gather_fusion = bf16[16384,128]{1,0:T(8,128)(2,1)} fusion(bf16[32768,128]{1,0:T(8,128)(2,1)} %param.8, s32[16384]{0:T(1024)S(1)} %broadcast_clamp_fusion), kind=kCustom, calls=%fused_computation | custom fusion | bytes 8454144 | tf_op jit(solution)/shard_map/jit(_take)/gather | solution.py:39
  379.4 1.8 collective-permute-start.13
  381.2 12.8 %fusion.3 = bf16[2048,128]{1,0:T(8,128)(2,1)S(1)} fusion(bf16[16384,128]{1,0:T(8,128)(2,1)} %gather_fusion, pred[2048,8]{1,0:T(8,128)(4,1)} %copy.15, pred[2048,8]{1,0:T(8,128)(4,1)S(1)} %copy.14), kind=kLoop, calls=%fused_computation.5 | loop fusion | flops 6029312 | bytes 4751360 | tf_op jit(solution)/shard_map/reduce_sum | solution.py:41
  394.9 4.7 all-to-all-start.1
  399.7 10.3 %collective-permute-done.13 = bf16[256,2048]{1,0:T(8,128)(2,1)} collective-permute-done((bf16[256,2048]{1,0:T(8,128)(2,1)}, bf16[256,2048]{1,0:T(8,128)(2,1)}, u32[]{:S(2)}, u32[]{:S(2)}) %collective-permute-start.13) | collective-permute-done | bytes 1048608 | tf_op jit(solution)/shard_map/ppermute | solution.py:14
  410.1 31.9 %all-to-all-done.1 = bf16[32,64,128]{2,1,0:T(8,128)(2,1)} async-done(((bf16[32,64,128]{2,1,0:T(8,128)(2,1)}), bf16[32,64,128]{2,1,0:T(8,128)(2,1)}, u32[]{:S(2)}, u32[]{:S(2)}) %all-to-all-start.1) | async-done | bytes 524320 | tf_op jit(solution)/shard_map/all_to_all | solution.py:45
  442.0 1.9 copy_bitcast_fusion
  444.0 2.5 constant_dynamic-update-slice_fusion.31
  446.5 3.3 constant_dynamic-update-slice_fusion.30
  449.8 2.3 constant_dynamic-update-slice_fusion.29
  452.1 2.3 constant_dynamic-update-slice_fusion.28
  454.4 2.3 constant_dynamic-update-slice_fusion.27
  456.8 2.3 constant_dynamic-update-slice_fusion.26
  459.1 2.3 constant_dynamic-update-slice_fusion.25
  461.4 2.4 constant_dynamic-update-slice_fusion.24
  463.8 2.4 constant_dynamic-update-slice_fusion.23
  466.2 2.3 constant_dynamic-update-slice_fusion.22
  468.5 2.3 constant_dynamic-update-slice_fusion.21
  470.8 2.3 constant_dynamic-update-slice_fusion.20
  473.2 2.3 constant_dynamic-update-slice_fusion.19
  475.5 1.1 constant_dynamic-update-slice_fusion.18
  476.6 1.1 constant_dynamic-update-slice_fusion.17
  477.7 1.1 constant_dynamic-update-slice_fusion.16
  478.8 2.3 constant_dynamic-update-slice_fusion.15
  481.1 2.3 constant_dynamic-update-slice_fusion.14
  483.4 2.3 constant_dynamic-update-slice_fusion.13
  485.7 2.3 constant_dynamic-update-slice_fusion.12
  488.0 1.1 constant_dynamic-update-slice_fusion.11
  489.1 1.1 constant_dynamic-update-slice_fusion.10
  490.2 1.0 constant_dynamic-update-slice_fusion.9
  491.2 1.1 constant_dynamic-update-slice_fusion.8
  492.4 1.1 constant_dynamic-update-slice_fusion.7
  493.5 1.1 constant_dynamic-update-slice_fusion.6
  494.5 1.1 constant_dynamic-update-slice_fusion.5
  495.6 1.1 constant_dynamic-update-slice_fusion.4
  496.7 1.1 constant_dynamic-update-slice_fusion.3
  497.8 1.1 constant_dynamic-update-slice_fusion.2
  498.8 1.1 constant_dynamic-update-slice_fusion.1
  500.0 1.1 constant_dynamic-update-slice_fusion
  501.1 8.6 %fusion.13 = f32[128]{0:T(128)S(1)} fusion(bf16[128,4096]{1,0:T(8,128)(2,1)} %all-gather.2.cloned.1.call-done, bf16[8192,2048]{1,0:T(8,128)(2,1)} %constant_dynamic-update-slice_fusion, s32[]{:T(128)S(6)} %select_n.70, f32[2048]{0:T(1024)S(1)} %convert_element_type.12, f32[2048]{0:T(1024)S(1)} %convert_element_type.5), kind=kOutput, calls=%fused_computation.9 | convolution fusion | flops 2148532224 | bytes 17842692 | tf_op jit(solution)/shard_map/dot_general | solution.py:60
  509.6 3.0 psum.7
  (74 shorter events, 9.8 us)
Async XLA Ops:
  6.5 30.3 %collective-permute-start = (bf16[256,2048]{1,0:T(8,128)(2,1)}, bf16[256,2048]{1,0:T(8,128)(2,1)S(1)}, u32[]{:S(2)}, u32[]{:S(2)}) collective-permute-start(bf16[256,2048]{1,0:T(8,128)(2,1)} %param.9), channel_id=1, source_target_pairs={{0,1},{1,2},{2,3},{3,4},{4,5},{5,6},{6,7},{7,8},{8,9},{9,10},{10,1... | collective-permute-start | bytes 3145736 | tf_op jit(solution)/shard_map/ppermute | solution.py:14
  36.9 27.9 %collective-permute-start.1 = (bf16[256,2048]{1,0:T(8,128)(2,1)S(1)}, bf16[256,2048]{1,0:T(8,128)(2,1)S(1)}, u32[]{:S(2)}, u32[]{:S(2)}) collective-permute-start(bf16[256,2048]{1,0:T(8,128)(2,1)S(1)} %collective-permute-done), channel_id=1, source_target_pairs={{0,1},{1,2},{2,3},{3,4},{4,5},{5,6},{6,7},{7,8},{8,9},{9,10},{10,1... | collective-permute-start | bytes 3145736 | tf_op jit(solution)/shard_map/ppermute | solution.py:14
  64.8 27.1 %collective-permute-start.2 = (bf16[256,2048]{1,0:T(8,128)(2,1)S(1)}, bf16[256,2048]{1,0:T(8,128)(2,1)S(1)}, u32[]{:S(2)}, u32[]{:S(2)}) collective-permute-start(bf16[256,2048]{1,0:T(8,128)(2,1)S(1)} %collective-permute-done.1), channel_id=1, source_target_pairs={{0,1},{1,2},{2,3},{3,4},{4,5},{5,6},{6,7},{7,8},{8,9},{9,10},{10,1... | collective-permute-start | bytes 3145736 | tf_op jit(solution)/shard_map/ppermute | solution.py:14
  91.8 1.0 copy-start.1
  92.8 26.2 %collective-permute-start.3 = (bf16[256,2048]{1,0:T(8,128)(2,1)S(1)}, bf16[256,2048]{1,0:T(8,128)(2,1)S(1)}, u32[]{:S(2)}, u32[]{:S(2)}) collective-permute-start(bf16[256,2048]{1,0:T(8,128)(2,1)S(1)} %collective-permute-done.2), channel_id=1, source_target_pairs={{0,1},{1,2},{2,3},{3,4},{4,5},{5,6},{6,7},{7,8},{8,9},{9,10},{10,1... | collective-permute-start | bytes 3145736 | tf_op jit(solution)/shard_map/ppermute | solution.py:14
  119.0 1.0 copy-start.3
  120.0 25.4 %collective-permute-start.4 = (bf16[256,2048]{1,0:T(8,128)(2,1)S(1)}, bf16[256,2048]{1,0:T(8,128)(2,1)S(1)}, u32[]{:S(2)}, u32[]{:S(2)}) collective-permute-start(bf16[256,2048]{1,0:T(8,128)(2,1)S(1)} %collective-permute-done.3), channel_id=1, source_target_pairs={{0,1},{1,2},{2,3},{3,4},{4,5},{5,6},{6,7},{7,8},{8,9},{9,10},{10,1... | collective-permute-start | bytes 3145736 | tf_op jit(solution)/shard_map/ppermute | solution.py:14
  145.4 1.0 copy-start.5
  146.4 24.5 %collective-permute-start.5 = (bf16[256,2048]{1,0:T(8,128)(2,1)S(1)}, bf16[256,2048]{1,0:T(8,128)(2,1)S(1)}, u32[]{:S(2)}, u32[]{:S(2)}) collective-permute-start(bf16[256,2048]{1,0:T(8,128)(2,1)S(1)} %collective-permute-done.4), channel_id=1, source_target_pairs={{0,1},{1,2},{2,3},{3,4},{4,5},{5,6},{6,7},{7,8},{8,9},{9,10},{10,1... | collective-permute-start | bytes 3145736 | tf_op jit(solution)/shard_map/ppermute | solution.py:14
  170.8 1.0 copy-start.7
  171.8 23.6 %collective-permute-start.6 = (bf16[256,2048]{1,0:T(8,128)(2,1)S(1)}, bf16[256,2048]{1,0:T(8,128)(2,1)S(1)}, u32[]{:S(2)}, u32[]{:S(2)}) collective-permute-start(bf16[256,2048]{1,0:T(8,128)(2,1)S(1)} %collective-permute-done.5), channel_id=1, source_target_pairs={{0,1},{1,2},{2,3},{3,4},{4,5},{5,6},{6,7},{7,8},{8,9},{9,10},{10,1... | collective-permute-start | bytes 3145736 | tf_op jit(solution)/shard_map/ppermute | solution.py:14
  195.5 1.0 copy-start.9
  196.5 22.8 %collective-permute-start.7 = (bf16[256,2048]{1,0:T(8,128)(2,1)S(1)}, bf16[256,2048]{1,0:T(8,128)(2,1)S(1)}, u32[]{:S(2)}, u32[]{:S(2)}) collective-permute-start(bf16[256,2048]{1,0:T(8,128)(2,1)S(1)} %collective-permute-done.6), channel_id=1, source_target_pairs={{0,1},{1,2},{2,3},{3,4},{4,5},{5,6},{6,7},{7,8},{8,9},{9,10},{10,1... | collective-permute-start | bytes 3145736 | tf_op jit(solution)/shard_map/ppermute | solution.py:14
  219.3 1.0 copy-start.11
  220.2 22.3 %collective-permute-start.8 = (bf16[256,2048]{1,0:T(8,128)(2,1)S(1)}, bf16[256,2048]{1,0:T(8,128)(2,1)S(1)}, u32[]{:S(2)}, u32[]{:S(2)}) collective-permute-start(bf16[256,2048]{1,0:T(8,128)(2,1)S(1)} %collective-permute-done.7), channel_id=1, source_target_pairs={{0,1},{1,2},{2,3},{3,4},{4,5},{5,6},{6,7},{7,8},{8,9},{9,10},{10,1... | collective-permute-start | bytes 3145736 | tf_op jit(solution)/shard_map/ppermute | solution.py:14
  242.5 1.1 copy-start.13
  243.5 22.4 %collective-permute-start.9 = (bf16[256,2048]{1,0:T(8,128)(2,1)S(1)}, bf16[256,2048]{1,0:T(8,128)(2,1)S(1)}, u32[]{:S(2)}, u32[]{:S(2)}) collective-permute-start(bf16[256,2048]{1,0:T(8,128)(2,1)S(1)} %collective-permute-done.8), channel_id=1, source_target_pairs={{0,1},{1,2},{2,3},{3,4},{4,5},{5,6},{6,7},{7,8},{8,9},{9,10},{10,1... | collective-permute-start | bytes 3145736 | tf_op jit(solution)/shard_map/ppermute | solution.py:14
  265.9 1.0 copy-start.15
  266.9 23.3 %collective-permute-start.10 = (bf16[256,2048]{1,0:T(8,128)(2,1)S(1)}, bf16[256,2048]{1,0:T(8,128)(2,1)S(1)}, u32[]{:S(2)}, u32[]{:S(2)}) collective-permute-start(bf16[256,2048]{1,0:T(8,128)(2,1)S(1)} %collective-permute-done.9), channel_id=1, source_target_pairs={{0,1},{1,2},{2,3},{3,4},{4,5},{5,6},{6,7},{7,8},{8,9},{9,10},{10,1... | collective-permute-start | bytes 3145736 | tf_op jit(solution)/shard_map/ppermute | solution.py:14
  290.2 29.3 %copy-start.17 = (bf16[256,2048]{1,0:T(8,128)(2,1)}, bf16[256,2048]{1,0:T(8,128)(2,1)S(1)}, u32[]{:S(2)}) copy-start(bf16[256,2048]{1,0:T(8,128)(2,1)S(1)} %collective-permute-done.10) | copy-start | bytes 3145732
  290.2 22.4 %collective-permute-start.11 = (bf16[256,2048]{1,0:T(8,128)(2,1)S(1)}, bf16[256,2048]{1,0:T(8,128)(2,1)}, u32[]{:S(2)}, u32[]{:S(2)}) collective-permute-start(bf16[256,2048]{1,0:T(8,128)(2,1)S(1)} %collective-permute-done.10), channel_id=1, source_target_pairs={{0,1},{1,2},{2,3},{3,4},{4,5},{5,6},{6,7},{7,8},{8,9},{9,10},{10,1... | collective-permute-start | bytes 3145736 | tf_op jit(solution)/shard_map/ppermute | solution.py:14
  292.0 19.0 %all-to-all-start = ((s32[32,1,512]{2,1,0:T(1,128)}), s32[32,1,512]{2,1,0:T(1,128)S(1)}, u32[]{:S(2)}, u32[]{:S(2)}) async-start(s32[32,1,512]{2,1,0:T(1,128)} %reshape.131), calls=%async_computation | async-start | bytes 131072 | tf_op jit(solution)/shard_map/all_to_all | solution.py:33
  299.8 13.7 %copy-start.21 = (pred[8]{0:T(512)(128)(4,1)}, pred[8]{0:T(512)(128)(4,1)S(1)}, u32[]{:S(2)}) copy-start(pred[8]{0:T(512)(128)(4,1)S(1)} %iota_compare_fusion) | copy-start | bytes 28
  312.6 66.9 %collective-permute-start.12 = (bf16[256,2048]{1,0:T(8,128)(2,1)}, bf16[256,2048]{1,0:T(8,128)(2,1)}, u32[]{:S(2)}, u32[]{:S(2)}) collective-permute-start(bf16[256,2048]{1,0:T(8,128)(2,1)} %collective-permute-done.11), channel_id=1, source_target_pairs={{0,1},{1,2},{2,3},{3,4},{4,5},{5,6},{6,7},{7,8},{8,9},{9,10},{10,1... | collective-permute-start | bytes 3145736 | tf_op jit(solution)/shard_map/ppermute | solution.py:14
  315.7 94.3 %copy-start.19 = (bf16[2048]{0:T(1024)(128)(2,1)S(1)}, bf16[2048]{0:T(1024)(128)(2,1)}, u32[]{:S(2)}) copy-start(bf16[2048]{0:T(1024)(128)(2,1)} %param.11) | copy-start | bytes 12292
  315.7 94.3 %copy-start.20 = (bf16[2048]{0:T(1024)(128)(2,1)S(1)}, bf16[2048]{0:T(1024)(128)(2,1)}, u32[]{:S(2)}) copy-start(bf16[2048]{0:T(1024)(128)(2,1)} %param.10) | copy-start | bytes 12292
  319.5 158.2 %copy-start = (bf16[256,2048]{1,0:T(8,128)(2,1)S(1)}, bf16[256,2048]{1,0:T(8,128)(2,1)}, u32[]{:S(2)}) copy-start(bf16[256,2048]{1,0:T(8,128)(2,1)} %param.9) | copy-start | bytes 3145732
  379.4 30.6 %collective-permute-start.13 = (bf16[256,2048]{1,0:T(8,128)(2,1)}, bf16[256,2048]{1,0:T(8,128)(2,1)}, u32[]{:S(2)}, u32[]{:S(2)}) collective-permute-start(bf16[256,2048]{1,0:T(8,128)(2,1)} %collective-permute-done.12), channel_id=1, source_target_pairs={{0,1},{1,2},{2,3},{3,4},{4,5},{5,6},{6,7},{7,8},{8,9},{9,10},{10,1... | collective-permute-start | bytes 3145736 | tf_op jit(solution)/shard_map/ppermute | solution.py:14
  394.9 47.0 %all-to-all-start.1 = ((bf16[32,64,128]{2,1,0:T(8,128)(2,1)}), bf16[32,64,128]{2,1,0:T(8,128)(2,1)}, u32[]{:S(2)}, u32[]{:S(2)}) async-start(bf16[32,64,128]{2,1,0:T(8,128)(2,1)} %bitcast.35), calls=%async_computation.1 | async-start | bytes 1048576 | tf_op jit(solution)/shard_map/all_to_all | solution.py:45
  399.7 101.4 %all-gather.2.cloned.1.call-start = ((), (), s32[]{:S(2)}) async-start(), calls=%async_computation.2 | async-start | bytes 1572864 | tf_op jit(solution)/shard_map/all_gather | solution.py:58
  410.0 34.0 %collective-permute-start.14 = (bf16[256,2048]{1,0:T(8,128)(2,1)}, bf16[256,2048]{1,0:T(8,128)(2,1)}, u32[]{:S(2)}, u32[]{:S(2)}) collective-permute-start(bf16[256,2048]{1,0:T(8,128)(2,1)} %collective-permute-done.13), channel_id=1, source_target_pairs={{0,1},{1,2},{2,3},{3,4},{4,5},{5,6},{6,7},{7,8},{8,9},{9,10},{10,1... | collective-permute-start | bytes 3145736 | tf_op jit(solution)/shard_map/ppermute | solution.py:14
  443.9 44.1 %copy-start.18 = (bf16[256,2048]{1,0:T(8,128)(2,1)S(1)}, bf16[256,2048]{1,0:T(8,128)(2,1)}, u32[]{:S(2)}) copy-start(bf16[256,2048]{1,0:T(8,128)(2,1)} %copy-done.17) | copy-start | bytes 3145732
  443.9 45.2 %copy-start.16 = (bf16[256,2048]{1,0:T(8,128)(2,1)S(1)}, bf16[256,2048]{1,0:T(8,128)(2,1)}, u32[]{:S(2)}) copy-start(bf16[256,2048]{1,0:T(8,128)(2,1)} %copy-done.15) | copy-start | bytes 3145732
  443.9 46.2 %copy-start.14 = (bf16[256,2048]{1,0:T(8,128)(2,1)S(1)}, bf16[256,2048]{1,0:T(8,128)(2,1)}, u32[]{:S(2)}) copy-start(bf16[256,2048]{1,0:T(8,128)(2,1)} %copy-done.13) | copy-start | bytes 3145732
  444.0 47.2 %copy-start.12 = (bf16[256,2048]{1,0:T(8,128)(2,1)S(1)}, bf16[256,2048]{1,0:T(8,128)(2,1)}, u32[]{:S(2)}) copy-start(bf16[256,2048]{1,0:T(8,128)(2,1)} %copy-done.11) | copy-start | bytes 3145732
  444.0 48.4 %copy-start.10 = (bf16[256,2048]{1,0:T(8,128)(2,1)S(1)}, bf16[256,2048]{1,0:T(8,128)(2,1)}, u32[]{:S(2)}) copy-start(bf16[256,2048]{1,0:T(8,128)(2,1)} %copy-done.9) | copy-start | bytes 3145732
  444.0 49.5 %copy-start.8 = (bf16[256,2048]{1,0:T(8,128)(2,1)S(1)}, bf16[256,2048]{1,0:T(8,128)(2,1)}, u32[]{:S(2)}) copy-start(bf16[256,2048]{1,0:T(8,128)(2,1)} %copy-done.7) | copy-start | bytes 3145732
  444.0 50.6 %copy-start.6 = (bf16[256,2048]{1,0:T(8,128)(2,1)S(1)}, bf16[256,2048]{1,0:T(8,128)(2,1)}, u32[]{:S(2)}) copy-start(bf16[256,2048]{1,0:T(8,128)(2,1)} %copy-done.5) | copy-start | bytes 3145732
  444.0 51.6 %copy-start.4 = (bf16[256,2048]{1,0:T(8,128)(2,1)S(1)}, bf16[256,2048]{1,0:T(8,128)(2,1)}, u32[]{:S(2)}) copy-start(bf16[256,2048]{1,0:T(8,128)(2,1)} %copy-done.3) | copy-start | bytes 3145732
  444.0 52.7 %copy-start.2 = (bf16[256,2048]{1,0:T(8,128)(2,1)S(1)}, bf16[256,2048]{1,0:T(8,128)(2,1)}, u32[]{:S(2)}) copy-start(bf16[256,2048]{1,0:T(8,128)(2,1)} %copy-done.1) | copy-start | bytes 3145732
Sparse Core Ops, SparseCore 0:
  444.0 4.9 all-gather.1
